TPU v7x, 32 devices: a whole 2x2x4 slice. The times are simulated.
32 devices in a mesh: dp: 2 (over x), expert: 16 (over z, y, core).
Axes of the slice: x: 2, y: 2, z: 4, core: 2. Of those that a mesh axis runs over, the one named last changes fastest.
Arguments:
- tokens: bfloat16 [4096, 2048], P(('dp', 'expert')), may hold values from -160 to 160
- router_weight: bfloat16 [2048, 16], replicated, may hold values from -0.25 to 0.25
- route_ids: int32 [4096, 2], P(('dp', 'expert')), may hold values from 0 to 15, as said below
- gate_weight: bfloat16 [16, 768, 2048], P('expert', 'dp'), may hold values from -0.125 to 0.125
- up_weight: bfloat16 [16, 768, 2048], P('expert', 'dp'), may hold values from -0.125 to 0.125
- down_weight: bfloat16 [16, 768, 2048], P('expert', 'dp'), may hold values from -0.21875 to 0.21875
Outputs:
- mixture: bfloat16 [4096, 2048], P(('dp', 'expert'))
- z_loss: float32 [], replicated
Inputs may be any that keep to these rules, and one draw needn't show every extreme that they name: `route_ids`: each row names 2 different experts; among the rows of one device no expert is named more than 20 times, and one expert is named exactly 20 times by the rows of every device.
All inputs are finite; a program needn't handle non-finite values.
Results may differ from a plain program's by a relative error of at most 0.0057.
Values may be sent and summed in bfloat16 or wider, within the bound.
No kernel may reach another device: no remote copies, remote signals or barrier semaphores. Data moves between devices by JAX's collectives and lax.ppermute only.
A program may use at most 64 MiB of HBM per device.

v0:
```python
import jax
import jax.numpy as jnp
from jax import lax
from jax.sharding import PartitionSpec as P


def slot_index(route_ids, experts, capacity):
    flat_ids = route_ids.reshape(-1)
    onehot = (flat_ids[:, None] == jnp.arange(experts, dtype=jnp.int32)[None, :]).astype(jnp.int32)
    before = jnp.cumsum(onehot, axis=0) - onehot
    position = jnp.sum(before * onehot, axis=1)
    return flat_ids * capacity + position


def on_device(tokens, router_weight, route_ids, gate_weight, up_weight, down_weight):
    rows_here, model_width = tokens.shape
    top_count = route_ids.shape[1]
    experts = router_weight.shape[1]
    owners = lax.axis_size("expert")
    local_experts = gate_weight.shape[0]
    capacity = 5 * rows_here * top_count // (4 * experts)
    logits = jnp.dot(tokens, router_weight, preferred_element_type=jnp.float32)
    log_total = jax.nn.logsumexp(logits, axis=1)
    local_sum = jnp.sum(log_total * log_total)
    chosen = jnp.take_along_axis(logits, route_ids, axis=1)
    route_weight = jax.nn.softmax(chosen, axis=1)
    slots = slot_index(route_ids, experts, capacity)
    pair_count = slots.shape[0]
    slot_match = slots[None, :] == jnp.arange(experts * capacity, dtype=jnp.int32)[:, None]
    token_of = jnp.arange(pair_count, dtype=jnp.int32) // top_count
    source_row = jnp.sum(jnp.where(slot_match, token_of[None, :], 0), axis=1)
    filled = jnp.any(slot_match, axis=1)
    dispatch = jnp.where(filled[:, None], tokens[source_row], jnp.zeros((), tokens.dtype))
    dispatch = dispatch.reshape(experts, capacity, model_width)
    received = lax.all_to_all(dispatch, "expert", split_axis=0, concat_axis=0, tiled=True)
    expert_rows = received.reshape(owners, local_experts, capacity, model_width)
    expert_rows = expert_rows.transpose(1, 0, 2, 3).reshape(
        local_experts, owners * capacity, model_width
    )
    gate_piece, up_piece = lax.all_gather((gate_weight, up_weight), "dp", axis=1, tiled=True)
    gate_val = jnp.einsum(
        "erd,efd->erf", expert_rows, gate_piece, preferred_element_type=jnp.float32
    )
    up_val = jnp.einsum("erd,efd->erf", expert_rows, up_piece, preferred_element_type=jnp.float32)
    hidden_all = (jax.nn.silu(gate_val) * up_val).astype(jnp.bfloat16)
    summed = jnp.einsum(
        "erf,efd->erd",
        hidden_all,
        lax.all_gather(down_weight, "dp", axis=1, tiled=True),
        preferred_element_type=jnp.float32,
    )
    expert_out = summed.astype(jnp.bfloat16)
    outgoing = expert_out.reshape(local_experts, owners, capacity, model_width)
    outgoing = outgoing.transpose(1, 0, 2, 3).reshape(experts, capacity, model_width)
    returned = lax.all_to_all(outgoing, "expert", split_axis=0, concat_axis=0, tiled=True)
    flat_rows = returned.reshape(experts * capacity, model_width)
    picked = flat_rows[slots].reshape(rows_here, top_count, model_width)
    mixed_out = jnp.sum(route_weight[:, :, None] * picked.astype(jnp.float32), axis=1).astype(
        jnp.bfloat16
    )
    total_sum = lax.psum(local_sum, ("dp", "expert"))
    token_total = rows_here * lax.axis_size("dp") * owners
    z_loss = total_sum / jnp.float32(token_total)
    return (mixed_out, z_loss)


def solution(mesh):
    in_specs = (
        P(("dp", "expert"), None),
        P(),
        P(("dp", "expert"), None),
        P("expert", "dp", None),
        P("expert", "dp", None),
        P("expert", "dp", None),
    )
    out_specs = (P(("dp", "expert"), None), P())
    return jax.shard_map(
        on_device, mesh=mesh, in_specs=in_specs, out_specs=out_specs, check_vma=False
    )
```

profile of v0, /device:TPU:0, one launch (start us, length us, event | category | flops | bytes accessed | tf_op | source)
XLA Modules:
  0.0 240.4 jit_solution(12554654109535446574)
XLA Ops:
  7.2 0.7 all-gather.4.cloned.1.call-update
  8.0 0.7 all-gather.6.cloned.1.call-update
  8.7 0.7 all-gather.8.cloned.1.call-update
  9.5 0.1 eq.39
  9.7 0.1 reshape.163
  9.8 0.6 reduce-window.6
  10.4 0.2 slice_reduce_fusion
  10.7 0.2 fusion.18
  10.9 0.1 select_reduce_fusion
  11.1 2.4 %gather_fusion = bf16[320,2048]{1,0:T(8,128)(2,1)S(1)} fusion(bf16[128,2048]{1,0:T(8,128)(2,1)S(1)} %copy-done, s32[1024]{0:T(1024)S(1)} %pad_clamp_fusion.1), kind=kCustom, calls=%fused_computation | custom fusion | bytes 2622720 | tf_op jit(solution)/shard_map/gather | solution.py:33
  13.5 0.3 gather.14
  14.0 0.2 broadcast_select_fusion
  14.2 43.1 %all_to_all.10 = bf16[16,20,2048]{2,1,0:T(8,128)(2,1)S(1)} all-to-all(bf16[16,20,2048]{2,1,0:T(8,128)(2,1)S(1)} %broadcast_select_fusion), channel_id=1, replica_groups=mesh['dp'=2,'expert'=16] {'expert'}, dimensions={0} | all-to-all | bytes 2621440 | tf_op jit(solution)/shard_map/all_to_all | solution.py:35
  57.3 0.3 reshape.165
  57.6 4.1 %fusion.4 = f32[320,768]{1,0:T(8,128)} fusion(bf16[320,2048]{1,0:T(8,128)(2,1)S(1)} %reshape.165, bf16[1,768,2048]{2,1,0:T(8,128)(2,1)} %all-gather.4.cloned.1.call-done), kind=kOutput, calls=%fused_computation.7 | convolution fusion | flops 1006632960 | bytes 5439488 | tf_op jit(solution)/shard_map/erd,efd->erf/dot_general | solution.py:41
  61.7 42.0 %all-gather.6.cloned.1.call-done = bf16[1,768,2048]{2,1,0:T(8,128)(2,1)} async-done(((bf16[1,384,2048]{2,1,0:T(8,128)(2,1)}), bf16[1,768,2048]{2,1,0:T(8,128)(2,1)}) %all-gather.6.cloned.1.call-update) | async-done | bytes 3145744 | tf_op jit(solution)/shard_map/all_gather | solution.py:40
  103.7 46.5 %all-gather.8.cloned.1.call-done = bf16[1,768,2048]{2,1,0:T(8,128)(2,1)} async-done(((bf16[1,384,2048]{2,1,0:T(8,128)(2,1)}), bf16[1,768,2048]{2,1,0:T(8,128)(2,1)}) %all-gather.8.cloned.1.call-update) | async-done | bytes 3145744 | tf_op jit(solution)/shard_map/all_gather | solution.py:49
  150.2 5.8 %fusion.6 = bf16[320,2048]{1,0:T(8,128)(2,1)S(1)} fusion(bf16[1,768,2048]{2,1,0:T(8,128)(2,1)} %all-gather.8.cloned.1.call-done, bf16[320,2048]{1,0:T(8,128)(2,1)S(1)} %reshape.165, bf16[1,768,2048]{2,1,0:T(8,128)(2,1)} %all-gather.6.cloned.1.call-done, f32[320,768]{1,0:T(8,128)} %fusion.4), kind=kOutput, calls=%fused_computation.9 | convolution fusion | flops 2015395840 | bytes 9895936 | tf_op jit(solution)/shard_map/erf,efd->erd/dot_general | solution.py:46
  155.9 1.3 reshape_transpose_reshape.4
  157.3 5.8 %all-to-all-start.1 = ((bf16[16,20,2048]{2,1,0:T(8,128)(2,1)}), bf16[16,20,2048]{2,1,0:T(8,128)(2,1)S(1)}, u32[]{:S(2)}, u32[]{:S(2)}) async-start(bf16[16,20,2048]{2,1,0:T(8,128)(2,1)} %reshape_transpose_reshape.4), calls=%async_computation.1 | async-start | bytes 3145728 | tf_op jit(solution)/shard_map/all_to_all | solution.py:55
  163.0 0.3 fusion.28
  163.3 0.6 multiply_reduce_fusion.1
  163.9 56.2 %psum.7 = f32[]{:T(128)} all-reduce(f32[]{:T(128)} %multiply_reduce_fusion.1), channel_id=1, replica_groups=mesh['dp'=2,'expert'=16] {'dp','expert'}, use_global_device_ids=true, to_apply=%region_11.12 | all-reduce | flops 1 | bytes 8 | tf_op jit(solution)/shard_map/psum | solution.py:61
  220.1 0.1 copy.33
  220.2 0.1 mul.55
  220.5 0.1 reshape.187
  220.6 2.0 gather_fusion.2
  222.6 0.1 reshape.190
  223.7 0.3 reshape.169
  224.0 2.3 gather_fusion.1
  226.4 2.4 reshape.170
  228.8 3.9 %multiply_reduce_fusion = bf16[128,2048]{1,0:T(8,128)(2,1)} fusion(f32[128,2,2048]{2,1,0:T(2,128)S(1)} %reshape.170, f32[128,2]{1,0:T(8,128)S(1)} %copy.29), kind=kLoop, calls=%fused_computation.10 | loop fusion | flops 786432 | bytes 2622464 | tf_op jit(solution)/shard_map/reduce_sum | solution.py:58
  (32 shorter events, 0.9 us)
Async XLA Ops:
  7.2 3.9 %copy-start = (bf16[128,2048]{1,0:T(8,128)(2,1)S(1)}, bf16[128,2048]{1,0:T(8,128)(2,1)}, u32[]{:S(2)}) copy-start(bf16[128,2048]{1,0:T(8,128)(2,1)} %param.6) | copy-start | bytes 1572868
  7.2 50.4 %all-gather.4.cloned.1.call-start = ((), (), s32[]{:S(2)}) async-start(), calls=%async_computation.2 | async-start | bytes 4718592 | tf_op jit(solution)/shard_map/all_gather | solution.py:40
  7.9 1.5 copy-start.2
  7.9 95.8 %all-gather.6.cloned.1.call-start = ((), (), s32[]{:S(2)}) async-start(), calls=%async_computation.3 | async-start | bytes 4718592 | tf_op jit(solution)/shard_map/all_gather | solution.py:40
  8.7 141.5 %all-gather.8.cloned.1.call-start = ((), (), s32[]{:S(2)}) async-start(), calls=%async_computation.4 | async-start | bytes 4718592 | tf_op jit(solution)/shard_map/all_gather | solution.py:49
  157.3 5.8 %copy-start.1 = (bf16[2048,16]{0,1:T(8,128)(2,1)S(1)}, bf16[2048,16]{0,1:T(8,128)(2,1)}, u32[]{:S(2)}) copy-start(bf16[2048,16]{0,1:T(8,128)(2,1)} %param.7) | copy-start | bytes 196612
  157.3 66.5 %all-to-all-start.1 = ((bf16[16,20,2048]{2,1,0:T(8,128)(2,1)}), bf16[16,20,2048]{2,1,0:T(8,128)(2,1)S(1)}, u32[]{:S(2)}, u32[]{:S(2)}) async-start(bf16[16,20,2048]{2,1,0:T(8,128)(2,1)} %reshape_transpose_reshape.4), calls=%async_computation.1 | async-start | bytes 3145728 | tf_op jit(solution)/shard_map/all_to_all | solution.py:55
Sparse Core Ops, SparseCore 0:
  9.5 47.6 all-gather.3
  58.7 44.8 all-gather.5
  105.2 44.8 all-gather.7
where the time goes:
time: 241 us; the launch traced here: 240 us
  blocking collectives  99.3 us (41%)
  waiting for transfers between devices  90.6 us (38%)
  between operations  15.8 us (7%)
  local copies, waits for them, and re-layouts  12.9 us (5%)
  matrix products  10.1 us (4%)
  other arithmetic  5.91 us (2%)
  starting transfers between devices  5.87 us (2%)
    psum x1, blocking collectives, on_device(): total_sum = lax.psum(local_sum, ('dp', 'expert'))  56.2 us
    all_gather x1, waiting for transfers between devices, on_device(): lax.all_gather(down_weight, 'dp', axis=1, tiled=True)  46.5 us
    all_to_all x1, blocking collectives, on_device(): lax.all_to_all(dispatch, 'expert', split_axis=0, concat_axis=0, tiled=True)  43.1 us
    all_gather x2, waiting for transfers between devices, on_device(): lax.all_gather((gate_weight, up_weight), 'dp', axis=1, tiled=True)  42 us
    dot_general x1, matrix products, on_device(): jnp.einsum('erf,efd->erd', hidden_all, lax.all_gather(down_weight, 'dp',...  5.77 us
    all_to_all x1, starting transfers between devices, on_device(): lax.all_to_all(outgoing, 'expert', split_axis=0, concat_axis=0, tiled=True)  5.75 us
  transfers between devices with their start and end apart: 4, of which 2 were waited for; matrix products, arithmetic and copies ran while one was open for 5% of the time, Pallas kernels for 0%

commit v1 on v0

--- a/solution.py
+++ b/solution.py
@@ -2,6 +2,18 @@
 import jax.numpy as jnp
 from jax import lax
 from jax.sharding import PartitionSpec as P
+
+
+def summed_around(x, axis, dim, product):
+    peers, index, span = (lax.axis_size(axis), lax.axis_index(axis), x.shape[dim])
+    right = [(i, (i + 1) % peers) for i in range(peers)]
+    current, so_far = (x, None)
+    for lap in range(peers):
+        coming = lax.ppermute(current, axis, right) if lap < peers - 1 else None
+        absorb = product(current, (index - lap) % peers * span)
+        so_far = absorb if so_far is None else so_far + absorb
+        current = coming
+    return so_far
 
 
 def slot_index(route_ids, experts, capacity):
@@ -43,11 +55,16 @@
     )
     up_val = jnp.einsum("erd,efd->erf", expert_rows, up_piece, preferred_element_type=jnp.float32)
     hidden_all = (jax.nn.silu(gate_val) * up_val).astype(jnp.bfloat16)
-    summed = jnp.einsum(
-        "erf,efd->erd",
-        hidden_all,
-        lax.all_gather(down_weight, "dp", axis=1, tiled=True),
-        preferred_element_type=jnp.float32,
+    summed = summed_around(
+        down_weight,
+        "dp",
+        1,
+        lambda part, start: jnp.einsum(
+            "erf,efd->erd",
+            lax.dynamic_slice_in_dim(hidden_all, start, part.shape[1], axis=2),
+            part,
+            preferred_element_type=jnp.float32,
+        ),
     )
     expert_out = summed.astype(jnp.bfloat16)
     outgoing = expert_out.reshape(local_experts, owners, capacity, model_width)

time: 241 us -> 227 us (0.942)
  blocking collectives: 99.3 us -> 56.2 us
  waiting for transfers between devices: 90.6 us -> 109 us
  starting transfers between devices: 5.87 us -> 14.8 us
    all_gather x1 -> x0, waiting for transfers between devices: 46.5 us -> none  [on_device(): lax.all_gather(down_weight, 'dp', axis=1, tiled=True)]
    all_to_all x1 -> x0, blocking collectives: 43.1 us -> none  [on_device(): lax.all_to_all(dispatch, 'expert', split_axis=0, concat_axis=0, tiled=True)]
    all_gather x2, waiting for transfers between devices: 42 us -> 76.8 us  [on_device(): lax.all_gather((gate_weight, up_weight), 'dp', axis=1, tiled=True)]
    all_to_all x0 -> x1, waiting for transfers between devices: none -> 30.3 us  [on_device(): lax.all_to_all(dispatch, 'expert', split_axis=0, concat_axis=0, tiled=True)]
    all_to_all x0 -> x1, starting transfers between devices: none -> 7.41 us  [on_device(): lax.all_to_all(dispatch, 'expert', split_axis=0, concat_axis=0, tiled=True)]
    dot_general x1 -> x3, matrix products: 5.77 us -> 6.53 us  [the longest x1 3.39 us: on_device(): jnp.einsum('erd,efd->erf', expert_rows, up_piece, preferred_element_type=...]
  transfers between devices with their start and end apart: 4 -> 5, of which waited for: 2 -> 3; matrix products, arithmetic and copies ran while one was open for 5% -> 8% of each run, Pallas kernels for 0% -> 0%
where the time goes in v1:
time: 227 us
  waiting for transfers between devices  109 us (48%)
  blocking collectives  56.2 us (25%)
  between operations  16.1 us (7%)
  starting transfers between devices  14.8 us (7%)
  local copies, waits for them, and re-layouts  12.9 us (6%)
  matrix products  10.9 us (5%)
  other arithmetic  7.15 us (3%)
    all_gather x2, waiting for transfers between devices, on_device(): lax.all_gather((gate_weight, up_weight), 'dp', axis=1, tiled=True)  76.8 us
    psum x1, blocking collectives, on_device(): total_sum = lax.psum(local_sum, ('dp', 'expert'))  56.2 us
    all_to_all x1, waiting for transfers between devices, on_device(): lax.all_to_all(dispatch, 'expert', split_axis=0, concat_axis=0, tiled=True)  30.3 us
    all_to_all x1, starting transfers between devices, on_device(): lax.all_to_all(dispatch, 'expert', split_axis=0, concat_axis=0, tiled=True)  7.41 us
    all_to_all x1, starting transfers between devices, on_device(): lax.all_to_all(outgoing, 'expert', split_axis=0, concat_axis=0, tiled=True)  5.75 us
  transfers between devices with their start and end apart: 5, of which 3 were waited for; matrix products, arithmetic and copies ran while one was open for 8% of the time, Pallas kernels for 0%

profile of v1, /device:TPU:0, one launch (start us, length us, event | category | flops | bytes accessed | tf_op | source)
XLA Modules:
  0.0 226.5 jit_solution(14715360825186800267)
XLA Ops:
  7.2 0.7 all-gather.3.cloned.1.call-update
  8.0 0.7 all-gather.5.cloned.1.call-update
  8.9 0.1 reshape.172
  9.1 0.6 reduce-window.6
  9.7 0.2 slice_reduce_fusion
  10.0 0.2 fusion.14
  10.2 0.1 select_reduce_fusion
  10.4 2.4 %gather_fusion = bf16[320,2048]{1,0:T(8,128)(2,1)S(1)} fusion(bf16[128,2048]{1,0:T(8,128)(2,1)S(1)} %copy-done, s32[1024]{0:T(1024)S(1)} %pad_clamp_fusion.1), kind=kCustom, calls=%fused_computation | custom fusion | bytes 2622720 | tf_op jit(solution)/shard_map/gather | solution.py:45
  12.8 0.3 gather.14
  13.2 1.4 broadcast_select_fusion
  14.6 7.4 %all-to-all-start = ((bf16[16,20,2048]{2,1,0:T(8,128)(2,1)}), bf16[16,20,2048]{2,1,0:T(8,128)(2,1)S(1)}, u32[]{:S(2)}, u32[]{:S(2)}) async-start(bf16[16,20,2048]{2,1,0:T(8,128)(2,1)} %broadcast_select_fusion), calls=%async_computation | async-start | bytes 3145728 | tf_op jit(solution)/shard_map/all_to_all | solution.py:47
  22.1 1.6 collective-permute-start
  23.6 30.3 %all-to-all-done = bf16[16,20,2048]{2,1,0:T(8,128)(2,1)S(1)} async-done(((bf16[16,20,2048]{2,1,0:T(8,128)(2,1)}), bf16[16,20,2048]{2,1,0:T(8,128)(2,1)S(1)}, u32[]{:S(2)}, u32[]{:S(2)}) %all-to-all-start) | async-done | bytes 1310752 | tf_op jit(solution)/shard_map/all_to_all | solution.py:47
  53.9 0.3 reshape.174
  54.2 34.7 %all-gather.3.cloned.1.call-done = bf16[1,768,2048]{2,1,0:T(8,128)(2,1)} async-done(((bf16[1,384,2048]{2,1,0:T(8,128)(2,1)}), bf16[1,768,2048]{2,1,0:T(8,128)(2,1)}) %all-gather.3.cloned.1.call-update) | async-done | bytes 3145744 | tf_op jit(solution)/shard_map/all_gather | solution.py:52
  88.9 4.2 %fusion.2 = f32[320,768]{1,0:T(8,128)} fusion(bf16[320,2048]{1,0:T(8,128)(2,1)S(1)} %reshape.174, bf16[1,768,2048]{2,1,0:T(8,128)(2,1)} %all-gather.3.cloned.1.call-done), kind=kOutput, calls=%fused_computation.5 | convolution fusion | flops 1006632960 | bytes 5439488 | tf_op jit(solution)/shard_map/erd,efd->erf/dot_general | solution.py:53
  93.1 42.1 %all-gather.5.cloned.1.call-done = bf16[1,768,2048]{2,1,0:T(8,128)(2,1)} async-done(((bf16[1,384,2048]{2,1,0:T(8,128)(2,1)}), bf16[1,768,2048]{2,1,0:T(8,128)(2,1)}) %all-gather.5.cloned.1.call-update) | async-done | bytes 3145744 | tf_op jit(solution)/shard_map/all_gather | solution.py:52
  135.2 3.4 %fusion.11 = bf16[320,768]{1,0:T(8,128)(2,1)S(1)} fusion(bf16[320,2048]{1,0:T(8,128)(2,1)S(1)} %reshape.174, bf16[1,768,2048]{2,1,0:T(8,128)(2,1)} %all-gather.5.cloned.1.call-done, f32[320,768]{1,0:T(8,128)} %fusion.2), kind=kOutput, calls=%fused_computation.15 | convolution fusion | flops 1008107520 | bytes 5931008 | tf_op jit(solution)/shard_map/erd,efd->erf/dot_general | solution.py:56
  138.6 0.8 fusion.6
  139.5 2.3 %fusion.4 = bf16[320,2048]{1,0:T(8,128)(2,1)S(1)} fusion(f32[320,2048]{1,0:T(8,128)S(1)} %fusion.6, bf16[1,384,2048]{2,1,0:T(8,128)(2,1)} %collective-permute-done, bf16[320,768]{1,0:T(8,128)(2,1)S(1)} %fusion.11, s32[]{:T(128)S(6)} %select_n.81), kind=kOutput, calls=%fused_computation.8 | convolution fusion | flops 504627200 | bytes 5750788 | tf_op jit(solution)/shard_map/erf,efd->erd/dot_general | solution.py:62
  141.8 1.3 reshape_transpose_reshape.4
  143.1 5.8 %all-to-all-start.1 = ((bf16[16,20,2048]{2,1,0:T(8,128)(2,1)}), bf16[16,20,2048]{2,1,0:T(8,128)(2,1)S(1)}, u32[]{:S(2)}, u32[]{:S(2)}) async-start(bf16[16,20,2048]{2,1,0:T(8,128)(2,1)} %reshape_transpose_reshape.4), calls=%async_computation.1 | async-start | bytes 3145728 | tf_op jit(solution)/shard_map/all_to_all | solution.py:72
  148.9 0.3 fusion.27
  149.2 0.6 multiply_reduce_fusion.1
  149.8 56.2 %psum.7 = f32[]{:T(128)} all-reduce(f32[]{:T(128)} %multiply_reduce_fusion.1), channel_id=1, replica_groups=mesh['dp'=2,'expert'=16] {'dp','expert'}, use_global_device_ids=true, to_apply=%region_11.12 | all-reduce | flops 1 | bytes 8 | tf_op jit(solution)/shard_map/psum | solution.py:78
  206.1 0.1 mul.63
  206.4 0.1 reshape.197
  206.5 2.0 gather_fusion.2
  209.6 0.3 reshape.179
  209.9 2.3 %gather_fusion.1 = bf16[256,2048]{1,0:T(8,128)(2,1)} fusion(bf16[320,2048]{1,0:T(8,128)(2,1)S(1)} %reshape.179, s32[1024]{0:T(1024)S(1)} %pad_clamp_fusion), kind=kCustom, calls=%fused_computation.1 | custom fusion | bytes 2098176 | tf_op jit(solution)/shard_map/gather | solution.py:74
  212.2 2.4 %reshape.180 = f32[128,2,2048]{2,1,0:T(2,128)S(1)} reshape(bf16[256,2048]{1,0:T(8,128)(2,1)} %gather_fusion.1) | data formatting | bytes 3145728 | tf_op jit(solution)/shard_map/convert_element_type | solution.py:75
  214.6 3.9 %multiply_reduce_fusion = bf16[128,2048]{1,0:T(8,128)(2,1)} fusion(f32[128,2,2048]{2,1,0:T(2,128)S(1)} %reshape.180, f32[128,2]{1,0:T(8,128)S(1)} %copy.29), kind=kLoop, calls=%fused_computation.9 | loop fusion | flops 786432 | bytes 2622464 | tf_op jit(solution)/shard_map/reduce_sum | solution.py:75
  (36 shorter events, 1.3 us)
Async XLA Ops:
  7.2 3.2 %copy-start = (bf16[128,2048]{1,0:T(8,128)(2,1)S(1)}, bf16[128,2048]{1,0:T(8,128)(2,1)}, u32[]{:S(2)}) copy-start(bf16[128,2048]{1,0:T(8,128)(2,1)} %param.6) | copy-start | bytes 1572868
  7.2 1.5 copy-start.3
  7.2 81.7 %all-gather.3.cloned.1.call-start = ((), (), s32[]{:S(2)}) async-start(), calls=%async_computation.2 | async-start | bytes 4718592 | tf_op jit(solution)/shard_map/all_gather | solution.py:52
  7.9 127.3 %all-gather.5.cloned.1.call-start = ((), (), s32[]{:S(2)}) async-start(), calls=%async_computation.3 | async-start | bytes 4718592 | tf_op jit(solution)/shard_map/all_gather | solution.py:52
  14.6 39.3 %all-to-all-start = ((bf16[16,20,2048]{2,1,0:T(8,128)(2,1)}), bf16[16,20,2048]{2,1,0:T(8,128)(2,1)S(1)}, u32[]{:S(2)}, u32[]{:S(2)}) async-start(bf16[16,20,2048]{2,1,0:T(8,128)(2,1)} %broadcast_select_fusion), calls=%async_computation | async-start | bytes 3145728 | tf_op jit(solution)/shard_map/all_to_all | solution.py:47
  22.1 117.4 %collective-permute-start = (bf16[1,384,2048]{2,1,0:T(8,128)(2,1)}, bf16[1,384,2048]{2,1,0:T(8,128)(2,1)}, u32[]{:S(2)}, u32[]{:S(2)}) collective-permute-start(bf16[1,384,2048]{2,1,0:T(8,128)(2,1)} %param.11), channel_id=1, source_target_pairs={{0,16},{16,0},{1,17},{17,1},{2,18},{18,2},{3,19},{19,3},{4,20},{20... | collective-permute-start | bytes 4718600 | tf_op jit(solution)/shard_map/ppermute | solution.py:12
  93.1 45.5 %copy-start.1 = (bf16[1,384,2048]{2,1,0:T(8,128)(2,1)S(1)}, bf16[1,384,2048]{2,1,0:T(8,128)(2,1)}, u32[]{:S(2)}) copy-start(bf16[1,384,2048]{2,1,0:T(8,128)(2,1)} %param.11) | copy-start | bytes 4718596
  143.1 5.8 %copy-start.2 = (bf16[2048,16]{0,1:T(8,128)(2,1)S(1)}, bf16[2048,16]{0,1:T(8,128)(2,1)}, u32[]{:S(2)}) copy-start(bf16[2048,16]{0,1:T(8,128)(2,1)} %param.7) | copy-start | bytes 196612
  143.1 66.5 %all-to-all-start.1 = ((bf16[16,20,2048]{2,1,0:T(8,128)(2,1)}), bf16[16,20,2048]{2,1,0:T(8,128)(2,1)S(1)}, u32[]{:S(2)}, u32[]{:S(2)}) async-start(bf16[16,20,2048]{2,1,0:T(8,128)(2,1)} %reshape_transpose_reshape.4), calls=%async_computation.1 | async-start | bytes 3145728 | tf_op jit(solution)/shard_map/all_to_all | solution.py:72
Sparse Core Ops, SparseCore 0:
  9.5 79.3 all-gather.2
  90.5 44.7 all-gather.4
